TPU v7x, 256 devices: a whole 4x4x8 slice. The times are simulated.
256 devices in a mesh: row: 8 (over y, core), col: 32 (over x, z).
Axes of the slice: x: 4, y: 4, z: 8, core: 2. Of those that a mesh axis runs over, the one named last changes fastest.
Arguments:
- normal: float32 [8, 8, 256, 2, 32, 256], P(None, 'row', None, None, 'col'), may hold values from -1.5 to 1.5
- panel_inverse: float32 [256, 256], replicated, as said below
- rhs: float32 [8, 8, 256, 512], P(None, 'row', None, 'col'), may hold values from -0.009765625 to 0.009765625
- shifts: float32 [4], replicated, may hold values from 16 to 128
Outputs:
- schur: float32 [8, 8, 256, 2, 32, 256], P(None, 'row', None, None, 'col')
- eliminated: float32 [8, 8, 256, 512], P(None, 'row', None, 'col')
- applied: float32 [8, 8, 256, 512], P(None, 'row', None, 'col')
Inputs may be any that keep to these rules, and one draw needn't show every extreme that they name: `panel_inverse`: lower triangular with positive diagonal entries.
All inputs are finite; a program needn't handle non-finite values.
Results may differ from a plain program's by a relative error of at most 0.000076.
Values sent between devices are 32-bit elements; how exact they have to be, the bound alone decides.
No kernel may reach another device: no remote copies, remote signals or barrier semaphores. Data moves between devices by JAX's collectives and lax.ppermute only.
A program may use at most 64 MiB of HBM per device.

v0:
```python
import jax
import jax.numpy as jnp
from jax import lax
from jax.sharding import Mesh
from jax.sharding import PartitionSpec as P

R = 128
COL = ("col_0", "col_1")


def from_root(array, axes, root):
    array = jnp.where(lax.axis_index(axes) == root, array, jnp.zeros_like(array))
    for axis in axes:
        array = lax.psum(array, axis)
    return array


def picked(array, axis, root):
    return lax.dynamic_index_in_dim(lax.all_gather(array, axis), root, 0, keepdims=False)


def copy_for_each(array, axis):
    copies = jnp.broadcast_to(array, (lax.axis_size(axis), *array.shape))
    return lax.all_to_all(copies, axis, split_axis=0, concat_axis=0, tiled=True)


def laid_out(blocks, dim):
    shape = list(blocks.shape[1:])
    shape[dim] *= blocks.shape[0]
    return jnp.moveaxis(blocks, 0, dim).reshape(shape)


def collect(array, axis, dim):
    blocks = copy_for_each(array, axis)
    return laid_out(blocks, dim)


def over_pieces(array, axis):
    blocks = lax.all_gather(array, axis)
    return blocks.sum(axis=0)


def pick_blocks(blocks, spacing, offset):
    grouped = blocks.reshape((blocks.shape[0] // spacing, spacing) + blocks.shape[1:])
    return lax.dynamic_index_in_dim(grouped, offset, 1, keepdims=False)


def shards(normal, panel_inverse, rhs, shifts):
    high = lax.Precision.HIGHEST
    row_index = lax.axis_index("row")
    col_index = lax.axis_index(COL)
    nrow = lax.axis_size("row")
    ncol = lax.axis_size(COL)
    spacing = ncol // nrow
    brows, nb, bcols = (normal.shape[0], normal.shape[2], normal.shape[3])
    narrow = rhs.shape[3]
    wide = narrow * ncol
    tile = normal.reshape(brows * nb, bcols * nb)
    owner = col_index % nrow
    offset = col_index // nrow
    early = lax.all_gather(rhs.reshape(brows, nb, narrow), COL, axis=2, tiled=True)
    local_panel = jnp.dot(
        tile[:, :nb], panel_inverse.T, precision=high, preferred_element_type=jnp.float32
    )
    panel = from_root(local_panel, COL, 0)
    chosen = pick_blocks(panel.reshape(brows, nb, nb), spacing, offset)
    crossed = picked(chosen, "row", owner).reshape(bcols * nb, nb)
    updated = tile - jnp.dot(panel, crossed.T, precision=high, preferred_element_type=jnp.float32)
    leading = picked(rhs[0, 0], "row", 0)
    first = jnp.dot(panel_inverse, leading, precision=high, preferred_element_type=jnp.float32)
    reduced = rhs.reshape(brows * nb, narrow) - jnp.dot(
        panel, first, precision=high, preferred_element_type=jnp.float32
    )
    reduced = reduced.reshape(brows, nb, narrow)
    reduced = reduced.at[0].set(jnp.where(row_index == 0, first, reduced[0]))
    first_all = collect(first, COL, 1)
    spread = early.reshape(brows * nb, wide) - jnp.dot(
        panel, first_all, precision=high, preferred_element_type=jnp.float32
    )
    spread = spread.reshape(brows, nb, wide)
    spread = spread.at[0].set(jnp.where(row_index == 0, first_all, spread[0]))
    scales = lax.dynamic_slice_in_dim(jnp.repeat(shifts, R), col_index * narrow, narrow)
    partial_value = lax.dot_general(
        updated,
        spread.reshape(brows * nb, wide),
        (((0,), (0,)), ((), ())),
        precision=high,
        preferred_element_type=jnp.float32,
    )
    totals = over_pieces(partial_value, "row")
    totals = totals.reshape(bcols, nb, ncol, narrow)
    arrived = lax.all_to_all(totals, COL, split_axis=2, concat_axis=2, tiled=True)
    arrived = arrived.reshape(bcols, nb, spacing, nrow, narrow)
    arrived = lax.dynamic_index_in_dim(arrived, row_index, 3, keepdims=False)
    product = jnp.transpose(arrived, (0, 2, 1, 3)).reshape(brows, nb, narrow)
    applied = product + reduced * scales[None, None, :]
    schur = updated.reshape(brows, 1, nb, bcols, 1, nb)
    return (schur, reduced.reshape(brows, 1, nb, narrow), applied.reshape(brows, 1, nb, narrow))


def solution(mesh):
    split = Mesh(mesh.devices.reshape(mesh.shape["row"], 4, 8), ("row", "col_0", "col_1"))
    placed = (P(None, "row", None, None, COL, None), P(), P(None, "row", None, COL), P())
    return jax.shard_map(
        shards,
        mesh=split,
        in_specs=placed,
        out_specs=(
            P(None, "row", None, None, COL, None),
            P(None, "row", None, COL),
            P(None, "row", None, COL),
        ),
        check_vma=False,
    )
```

profile of v0, /device:TPU:32, one launch (start us, length us, event | category | flops | bytes accessed | tf_op | source)
XLA Modules:
  0.0 382.1 jit_solution(8864626879516154711)
XLA Ops:
  8.1 15.9 %reduce.4 = f32[8,256,2,256]{3,2,1,0:T(2,128)} reduce(f32[8,1,256,2,1,256]{5,4,3,2,1,0:T(1,128)} %param.8, f32[]{:T(128)} %constant.112), dimensions={1,4}, to_apply=%param.8.reduce_sub_computation | reduce | bytes 8388612 | tf_op args[0]
  24.0 4.6 %copy.26 = f32[256,8,2,256]{3,1,2,0:T(8,128)} copy(f32[256,8,2,256]{3,2,1,0:T(2,128)} %bitcast.62) | data formatting | bytes 8388608
  28.5 4.8 %convolution_select_fusion = f32[2048,256]{1,0:T(8,128)} fusion(f32[256,256]{1,0:T(8,128)S(1)} %copy-done, f32[2048,512]{1,0:T(8,128)} %bitcast.58, pred[]{:T(512)S(6)} %eq.9), kind=kOutput, calls=%fused_computation.2 | convolution fusion | flops 1611137024 | bytes 4456449 | tf_op jit(solution)/shard_map/dot_general | solution.py:62
  33.4 66.4 %all-reduce.3.cloned.1.call-done = f32[2048,256]{1,0:T(8,128)} async-done(((f32[2048,256]{1,0:T(8,128)}), f32[2048,256]{1,0:T(8,128)}) %all-reduce.3.cloned.1.call-update) | async-done | bytes 2097168 | tf_op jit(solution)/shard_map/psum | solution.py:14
  99.9 0.5 all-gather.10.cloned.1.call-update
  100.5 95.7 %all-reduce.5.cloned.1.call-done = f32[2048,256]{1,0:T(8,128)} async-done(((f32[2048,256]{1,0:T(8,128)}), f32[2048,256]{1,0:T(8,128)}) %all-reduce.5.cloned.1.call-update) | async-done | bytes 2097168 | tf_op jit(solution)/shard_map/psum | solution.py:14
  196.3 1.9 constant_dynamic-slice_fusion.2
  198.2 13.1 %all-gather.1 = f32[8,1,256,16]{2,3,1,0:T(8,128)S(1)} all-gather(f32[1,1,256,16]{2,3,1,0:T(8,128)S(1)} %slice.56), channel_id=3, replica_groups=mesh['row'=8,'col_0'=4,'col_1'=8] {'row'}, dimensions={0}, use_global_device_ids=true | all-gather | bytes 147456 | tf_op jit(solution)/shard_map/all_gather | solution.py:19
  211.3 0.3 fusion.5
  211.5 0.9 broadcast_in_dim.11
  212.4 9.2 %all-to-all-start = ((f32[32,256,16]{1,2,0:T(8,128)}), f32[32,256,16]{1,2,0:T(8,128)S(1)}, u32[]{:S(2)}, u32[]{:S(2)}) async-start(f32[32,256,16]{1,2,0:T(8,128)} %broadcast_in_dim.11), calls=%async_computation | async-start | bytes 1048576 | tf_op jit(solution)/shard_map/all_to_all | solution.py:24
  221.6 0.2 all-gather.12.cloned.1.call-start
  221.9 17.9 %all-to-all-done = f32[32,256,16]{1,2,0:T(8,128)S(1)} async-done(((f32[32,256,16]{1,2,0:T(8,128)}), f32[32,256,16]{1,2,0:T(8,128)S(1)}, u32[]{:S(2)}, u32[]{:S(2)}) %all-to-all-start) | async-done | bytes 524320 | tf_op jit(solution)/shard_map/all_to_all | solution.py:24
  240.0 5.5 %copy.20 = f32[8,1,256,512]{3,2,0,1:T(8,128)} copy(f32[8,1,256,512]{2,3,1,0:T(8,128)} %all-gather.10.cloned.1.call-done) | data formatting | bytes 8388608 | tf_op jit(solution)/shard_map/all_gather | solution.py:61
  245.5 5.3 %bitcast_subtract_fusion = f32[2048,512]{1,0:T(8,128)S(1)} fusion(f32[8,1,256,512]{3,2,0,1:T(8,128)} %copy.20, f32[2048,256]{1,0:T(8,128)S(1)} %copy-done.2, f32[256,512]{0,1:T(8,128)S(1)} %bitcast.65), kind=kOutput, calls=%fused_computation | convolution fusion | flops 3222274048 | bytes 11010048 | tf_op jit(solution)/shard_map/dot_general | solution.py:77
  250.8 2.0 copy.34
  252.8 0.9 fusion.2
  253.7 1.1 constant_dynamic-slice_fusion.1
  254.8 5.5 %convolution_subtract_fusion = f32[2048,512]{1,0:T(8,128)S(1)} fusion(f32[2048,512]{1,0:T(8,128)} %bitcast.59, f32[2048,256]{1,0:T(8,128)S(1)} %copy-done.2, f32[512,256]{1,0:T(8,128)S(1)} %bitcast.66), kind=kOutput, calls=%fused_computation.1 | convolution fusion | flops 3222274048 | bytes 11010048 | tf_op jit(solution)/shard_map/dot_general | solution.py:68
  260.3 1.9 copy-done.1
  262.2 16.2 %fusion.6 = f32[512,512]{1,0:T(8,128)} fusion(f32[2048,512]{1,0:T(8,128)S(1)} %convolution_subtract_fusion, f32[2048,512]{1,0:T(8,128)} %bitcast.12), kind=kOutput, calls=%fused_computation.19 | convolution fusion | flops 6442450944 | bytes 9437184 | tf_op jit(solution)/shard_map/dot_general | solution.py:83
  278.5 47.7 %all-gather.12.cloned.1.call-done = f32[4096,512]{1,0:T(8,128)} async-done(((f32[512,512]{1,0:T(8,128)}), f32[4096,512]{1,0:T(8,128)}) %all-gather.12.cloned.1.call-update) | async-done | bytes 8388624 | tf_op jit(solution)/shard_map/all_gather | solution.py:39
  326.1 4.5 %reduce_sum.9 = f32[512,512]{1,0:T(8,128)S(1)} reduce(f32[8,512,512]{2,1,0:T(8,128)} %bitcast.63, f32[]{:T(128)} %constant.101.clone.1), dimensions={0}, to_apply=%region_2.3 | reduce | flops 1835008 | bytes 9437188 | tf_op jit(solution)/shard_map/reduce_sum | solution.py:40
  330.6 1.3 copy.22
  331.9 2.8 reshape.136
  334.8 10.1 %all-to-all-start.1 = ((f32[2,256,32,16]{1,0,3,2:T(2,128)}), f32[2,256,32,16]{1,0,3,2:T(2,128)S(1)}, u32[]{:S(2)}, u32[]{:S(2)}) async-start(f32[2,256,32,16]{1,0,3,2:T(2,128)} %reshape.136), calls=%async_computation.1 | async-start | bytes 2097152 | tf_op jit(solution)/shard_map/all_to_all | solution.py:92
  344.9 0.7 copy.27
  345.5 0.7 broadcast_bitcast_fusion
  346.3 2.8 convolution_subtract_fusion.1
  349.1 7.7 %reshape.148 = f32[8,1,256,2,1,256]{5,4,3,2,1,0:T(1,128)} reshape(f32[2048,512]{1,0:T(8,128)} %copy-done.1) | data formatting | bytes 8388608 | tf_op jit(solution)/shard_map/reshape | solution.py:97
  356.8 16.8 %all-to-all-done.1 = f32[2,256,32,16]{1,0,3,2:T(2,128)S(1)} async-done(((f32[2,256,32,16]{1,0,3,2:T(2,128)}), f32[2,256,32,16]{1,0,3,2:T(2,128)S(1)}, u32[]{:S(2)}, u32[]{:S(2)}) %all-to-all-start.1) | async-done | bytes 1048608 | tf_op jit(solution)/shard_map/all_to_all | solution.py:92
  373.8 0.7 bitcast_add_fusion
  (26 shorter events, 0.7 us)
Async XLA Ops:
  8.0 20.5 %copy-start = (f32[256,256]{1,0:T(8,128)S(1)}, f32[256,256]{1,0:T(8,128)}, u32[]{:S(2)}) copy-start(f32[256,256]{1,0:T(8,128)} %param.9) | copy-start | bytes 786436
  8.0 91.8 %all-reduce.3.cloned.1.call-start = ((), (), s32[]{:S(2)}) async-start(), calls=%async_computation.2 | async-start | bytes 4194304 | tf_op jit(solution)/shard_map/psum | solution.py:14
  28.5 169.6 %copy-start.3 = (f32[8,1,256,16]{2,3,1,0:T(8,128)S(1)}, f32[8,1,256,16]{2,3,1,0:T(8,128)}, u32[]{:S(2)}) copy-start(f32[8,1,256,16]{2,3,1,0:T(8,128)} %param.10) | copy-start | bytes 393220
  33.3 162.9 %all-reduce.5.cloned.1.call-start = ((), (), s32[]{:S(2)}) async-start(), calls=%async_computation.3 | async-start | bytes 4194304 | tf_op jit(solution)/shard_map/psum | solution.py:14
  99.9 140.1 %all-gather.10.cloned.1.call-start = ((), (), s32[]{:S(2)}) async-start(), calls=%async_computation.5 | async-start | bytes 4325376 | tf_op jit(solution)/shard_map/all_gather | solution.py:61
  100.4 153.2 %all-gather.8.cloned.1.call-start = ((), (), s32[]{:S(2)}) async-start(), calls=%async_computation.4 | async-start | bytes 4718592 | tf_op jit(solution)/shard_map/all_gather | solution.py:19
  212.4 27.3 %all-to-all-start = ((f32[32,256,16]{1,2,0:T(8,128)}), f32[32,256,16]{1,2,0:T(8,128)S(1)}, u32[]{:S(2)}, u32[]{:S(2)}) async-start(f32[32,256,16]{1,2,0:T(8,128)} %broadcast_in_dim.11), calls=%async_computation | async-start | bytes 1048576 | tf_op jit(solution)/shard_map/all_to_all | solution.py:24
  221.6 104.5 %all-gather.12.cloned.1.call-start = ((), (), s32[]{:S(2)}) async-start(), calls=%async_computation.6 | async-start | bytes 9437184 | tf_op jit(solution)/shard_map/all_gather | solution.py:39
  239.9 5.5 %copy-start.2 = (f32[2048,256]{1,0:T(8,128)S(1)}, f32[2048,256]{1,0:T(8,128)}, u32[]{:S(2)}) copy-start(f32[2048,256]{1,0:T(8,128)} %all-reduce.5.cloned.1.call-done) | copy-start | bytes 6291460
  260.3 2.0 copy-start.1
  334.8 38.8 %all-to-all-start.1 = ((f32[2,256,32,16]{1,0,3,2:T(2,128)}), f32[2,256,32,16]{1,0,3,2:T(2,128)S(1)}, u32[]{:S(2)}, u32[]{:S(2)}) async-start(f32[2,256,32,16]{1,0,3,2:T(2,128)} %reshape.136), calls=%async_computation.1 | async-start | bytes 2097152 | tf_op jit(solution)/shard_map/all_to_all | solution.py:92
  349.1 24.6 %copy-start.4 = (f32[8,256,16]{1,2,0:T(8,128)}, f32[8,256,16]{1,2,0:T(8,128)S(1)}, u32[]{:S(2)}) copy-start(f32[8,256,16]{1,2,0:T(8,128)S(1)} %fusion.4) | copy-start | bytes 393220
Sparse Core Ops, SparseCore 0:
  33.5 66.3 all-reduce.2
  102.2 94.0 all-reduce.4
Sparse Core Ops, SparseCore 1:
  102.9 92.5 all-gather.9
  198.2 34.9 all-gather.7
  278.6 47.5 all-gather.11
where the time goes:
time: 383 us; the launch traced here: 382 us
  waiting for transfers between devices  245 us (64%)
  matrix products  34.9 us (9%)
  local copies, waits for them, and re-layouts  31.6 us (8%)
  other arithmetic  22 us (6%)
  starting transfers between devices  19.6 us (5%)
  between operations  15.9 us (4%)
  blocking collectives  13.1 us (3%)
    psum x2, waiting for transfers between devices, from_root(): array = lax.psum(array, axis)  162 us
    all_gather x1, waiting for transfers between devices, over_pieces(): blocks = lax.all_gather(array, axis)  47.7 us
    all_to_all x1, waiting for transfers between devices, copy_for_each(): return lax.all_to_all(copies, axis, split_axis=0, concat_axis=0, tiled=True)  17.9 us
    all_to_all x1, waiting for transfers between devices, shards(): lax.all_to_all(totals, COL, split_axis=2, concat_axis=2, tiled=True)  16.8 us
    dot_general x1, matrix products, shards(): lax.dot_general(updated, spread.reshape(brows * nb, wide), (((0,), (0,)),...  16.2 us
    unnamed x1, other arithmetic  15.9 us
    all_gather x1, blocking collectives, picked(): lax.all_gather(array, axis)  13.1 us
    all_to_all x1, starting transfers between devices, shards(): lax.all_to_all(totals, COL, split_axis=2, concat_axis=2, tiled=True)  10.1 us
  transfers between devices with their start and end apart: 7, of which 5 were waited for; matrix products, arithmetic and copies ran while one was open for 8% of the time, Pallas kernels for 0%

commit v1 on v0

--- a/solution.py
+++ b/solution.py
@@ -11,7 +11,8 @@
 def from_root(array, axes, root):
     array = jnp.where(lax.axis_index(axes) == root, array, jnp.zeros_like(array))
     for axis in axes:
-        array = lax.psum(array, axis)
+        parts = lax.all_gather(array, axis, axis=0, tiled=False)
+        array = parts.sum(axis=0)
     return array
 
 

time: 383 us -> 552 us (1.44)
  waiting for transfers between devices: 245 us -> 407 us
  other arithmetic: 22 us -> 34.7 us
    all_gather x0 -> x2, waiting for transfers between devices: none -> 260 us  [from_root(): parts = lax.all_gather(array, axis, axis=0, tiled=False)]
    psum x2 -> x0, waiting for transfers between devices: 162 us -> none  [from_root(): array = lax.psum(array, axis)]
    all_gather x1, waiting for transfers between devices: 0.03 us -> 37.2 us  [shards(): lax.all_gather(rhs.reshape(brows, nb, narrow), COL, axis=2, tiled=True)]
    all_gather x1, waiting for transfers between devices: 0.01 us -> 19.9 us  [picked(): lax.all_gather(array, axis)]
    reduce_sum x0 -> x2, other arithmetic: none -> 12.7 us  [from_root(): array = parts.sum(axis=0)]
  transfers between devices with their start and end apart: 7 -> 7, of which waited for: 5 -> 7; matrix products, arithmetic and copies ran while one was open for 8% -> 6% of each run, Pallas kernels for 0% -> 0%
where the time goes in v1:
time: 552 us; the launch traced here: 551 us
  waiting for transfers between devices  407 us (74%)
  other arithmetic  34.7 us (6%)
  matrix products  33.9 us (6%)
  local copies, waits for them, and re-layouts  29.1 us (5%)
  starting transfers between devices  19.6 us (4%)
  between operations  14 us (3%)
  blocking collectives  13.1 us (2%)
    all_gather x2, waiting for transfers between devices, from_root(): parts = lax.all_gather(array, axis, axis=0, tiled=False)  260 us
    all_gather x1, waiting for transfers between devices, over_pieces(): blocks = lax.all_gather(array, axis)  52.3 us
    all_gather x1, waiting for transfers between devices, shards(): lax.all_gather(rhs.reshape(brows, nb, narrow), COL, axis=2, tiled=True)  37.2 us
    all_gather x1, waiting for transfers between devices, picked(): lax.all_gather(array, axis)  19.9 us
    all_to_all x1, waiting for transfers between devices, shards(): lax.all_to_all(totals, COL, split_axis=2, concat_axis=2, tiled=True)  18.9 us
    all_to_all x1, waiting for transfers between devices, copy_for_each(): return lax.all_to_all(copies, axis, split_axis=0, concat_axis=0, tiled=True)  18.3 us
    dot_general x1, matrix products, shards(): lax.dot_general(updated, spread.reshape(brows * nb, wide), (((0,), (0,)),...  16.2 us
    unnamed x1, other arithmetic  15.9 us
  transfers between devices with their start and end apart: 7, of which 7 were waited for; matrix products, arithmetic and copies ran while one was open for 6% of the time, Pallas kernels for 0%

profile of v1, /device:TPU:32, one launch (start us, length us, event | category | flops | bytes accessed | tf_op | source)
XLA Modules:
  0.0 551.3 jit_solution(8926751303388959762)
XLA Ops:
  7.2 15.9 %reduce.4 = f32[8,256,2,256]{3,2,1,0:T(2,128)} reduce(f32[8,1,256,2,1,256]{5,4,3,2,1,0:T(1,128)} %param.8, f32[]{:T(128)} %constant.112), dimensions={1,4}, to_apply=%param.8.reduce_sub_computation | reduce | bytes 8388612 | tf_op args[0]
  23.1 4.6 copy.33
  27.7 4.7 convolution_select_fusion
  32.5 88.3 %all-gather.12.cloned.1.call-done = f32[8192,256]{1,0:T(8,128)} async-done(((f32[2048,256]{1,0:T(8,128)}), f32[8192,256]{1,0:T(8,128)}) %all-gather.12.cloned.1.call-update) | async-done | bytes 8388624 | tf_op jit(solution)/shard_map/all_gather | solution.py:14
  120.8 5.5 %reduce_sum.27 = f32[2048,256]{1,0:T(8,128)} reduce(f32[4,2048,256]{2,1,0:T(8,128)} %bitcast.67, f32[]{:T(128)} %constant.101.clone.1), dimensions={0}, to_apply=%region_0.1 | reduce | flops 1572864 | bytes 10485764 | tf_op jit(solution)/shard_map/reduce_sum | solution.py:15
  126.4 0.7 all-gather.18.cloned.1.call-update
  127.2 171.3 %all-gather.14.cloned.1.call-done = f32[16384,256]{1,0:T(8,128)} async-done(((f32[2048,256]{1,0:T(8,128)}), f32[16384,256]{1,0:T(8,128)}) %all-gather.14.cloned.1.call-update) | async-done | bytes 16777232 | tf_op jit(solution)/shard_map/all_gather | solution.py:14
  298.5 7.1 %reduce_sum.28 = f32[2048,256]{1,0:T(8,128)S(1)} reduce(f32[8,2048,256]{2,1,0:T(8,128)} %bitcast.64, f32[]{:T(128)} %constant.101.clone.1), dimensions={0}, to_apply=%region_1.2 | reduce | flops 3670016 | bytes 18874372 | tf_op jit(solution)/shard_map/reduce_sum | solution.py:15
  305.6 0.8 constant_dynamic-slice_fusion.2
  306.5 13.1 %all-gather.3 = f32[8,1,256,16]{2,3,1,0:T(8,128)S(1)} all-gather(f32[1,1,256,16]{2,3,1,0:T(8,128)S(1)} %slice.56), channel_id=5, replica_groups=mesh['row'=8,'col_0'=4,'col_1'=8] {'row'}, dimensions={0}, use_global_device_ids=true | all-gather | bytes 147456 | tf_op jit(solution)/shard_map/all_gather | solution.py:20
  319.8 0.9 broadcast_in_dim.11
  320.7 9.2 %all-to-all-start = ((f32[32,256,16]{1,2,0:T(8,128)}), f32[32,256,16]{1,2,0:T(8,128)S(1)}, u32[]{:S(2)}, u32[]{:S(2)}) async-start(f32[32,256,16]{1,2,0:T(8,128)} %broadcast_in_dim.11), calls=%async_computation | async-start | bytes 1048576 | tf_op jit(solution)/shard_map/all_to_all | solution.py:25
  330.2 18.3 %all-to-all-done = f32[32,256,16]{1,2,0:T(8,128)S(1)} async-done(((f32[32,256,16]{1,2,0:T(8,128)}), f32[32,256,16]{1,2,0:T(8,128)S(1)}, u32[]{:S(2)}, u32[]{:S(2)}) %all-to-all-start) | async-done | bytes 524320 | tf_op jit(solution)/shard_map/all_to_all | solution.py:25
  348.6 37.2 %all-gather.18.cloned.1.call-done = f32[8,1,256,512]{2,3,1,0:T(8,128)} async-done(((f32[8,1,256,16]{2,3,1,0:T(8,128)}), f32[8,1,256,512]{2,3,1,0:T(8,128)}) %all-gather.18.cloned.1.call-update) | async-done | bytes 4194320 | tf_op jit(solution)/shard_map/all_gather | solution.py:62
  385.9 5.3 copy.27
  391.2 5.3 bitcast_subtract_fusion
  396.5 2.0 copy.39
  398.6 0.9 fusion.2
  399.4 19.9 %all-gather.16.cloned.1.call-done = f32[16,1,256,256]{3,2,1,0:T(8,128)} async-done(((f32[2,1,256,256]{3,2,1,0:T(8,128)}), f32[16,1,256,256]{3,2,1,0:T(8,128)}) %all-gather.16.cloned.1.call-update) | async-done | bytes 4194320 | tf_op jit(solution)/shard_map/all_gather | solution.py:20
  419.3 1.1 constant_dynamic-slice_fusion.1
  420.4 5.5 convolution_subtract_fusion
  425.9 2.0 copy-done.2
  427.8 16.2 %fusion.6 = f32[512,512]{1,0:T(8,128)} fusion(f32[2048,512]{1,0:T(8,128)S(1)} %convolution_subtract_fusion, f32[2048,512]{1,0:T(8,128)} %bitcast.14), kind=kOutput, calls=%fused_computation.19 | convolution fusion | flops 6442450944 | bytes 9437184 | tf_op jit(solution)/shard_map/dot_general | solution.py:84
  444.1 52.3 %all-gather.20.cloned.1.call-done = f32[4096,512]{1,0:T(8,128)} async-done(((f32[512,512]{1,0:T(8,128)}), f32[4096,512]{1,0:T(8,128)}) %all-gather.20.cloned.1.call-update) | async-done | bytes 8388624 | tf_op jit(solution)/shard_map/all_gather | solution.py:40
  496.4 4.5 reduce_sum.29
  500.9 1.3 copy.29
  502.2 2.8 reshape.136
  505.1 10.1 %all-to-all-start.1 = ((f32[2,256,32,16]{1,0,3,2:T(2,128)}), f32[2,256,32,16]{1,0,3,2:T(2,128)S(1)}, u32[]{:S(2)}, u32[]{:S(2)}) async-start(f32[2,256,32,16]{1,0,3,2:T(2,128)} %reshape.136), calls=%async_computation.1 | async-start | bytes 2097152 | tf_op jit(solution)/shard_map/all_to_all | solution.py:93
  515.3 1.8 convolution_subtract_fusion.1
  517.2 7.7 %reshape.150 = f32[8,1,256,2,1,256]{5,4,3,2,1,0:T(1,128)} reshape(f32[2048,512]{1,0:T(8,128)} %copy-done.2) | data formatting | bytes 8388608 | tf_op jit(solution)/shard_map/reshape | solution.py:98
  525.0 18.9 %all-to-all-done.1 = f32[2,256,32,16]{1,0,3,2:T(2,128)S(1)} async-done(((f32[2,256,32,16]{1,0,3,2:T(2,128)}), f32[2,256,32,16]{1,0,3,2:T(2,128)S(1)}, u32[]{:S(2)}, u32[]{:S(2)}) %all-to-all-start.1) | async-done | bytes 1048608 | tf_op jit(solution)/shard_map/all_to_all | solution.py:93
  544.1 0.7 bitcast_add_fusion
  (30 shorter events, 1.3 us)
Async XLA Ops:
  7.2 20.5 %copy-start = (f32[256,256]{1,0:T(8,128)S(1)}, f32[256,256]{1,0:T(8,128)}, u32[]{:S(2)}) copy-start(f32[256,256]{1,0:T(8,128)} %param.9) | copy-start | bytes 786436
  7.2 113.6 %all-gather.12.cloned.1.call-start = ((), (), s32[]{:S(2)}) async-start(), calls=%async_computation.2 | async-start | bytes 10485760 | tf_op jit(solution)/shard_map/all_gather | solution.py:14
  32.5 266.0 %all-gather.14.cloned.1.call-start = ((), (), s32[]{:S(2)}) async-start(), calls=%async_computation.3 | async-start | bytes 18874368 | tf_op jit(solution)/shard_map/all_gather | solution.py:14
  126.4 259.5 %all-gather.18.cloned.1.call-start = ((), (), s32[]{:S(2)}) async-start(), calls=%async_computation.5 | async-start | bytes 4325376 | tf_op jit(solution)/shard_map/all_gather | solution.py:62
  127.1 292.2 %all-gather.16.cloned.1.call-start = ((), (), s32[]{:S(2)}) async-start(), calls=%async_computation.4 | async-start | bytes 4718592 | tf_op jit(solution)/shard_map/all_gather | solution.py:20
  298.5 8.0 %copy-start.3 = (f32[8,1,256,16]{2,3,1,0:T(8,128)S(1)}, f32[8,1,256,16]{2,3,1,0:T(8,128)}, u32[]{:S(2)}) copy-start(f32[8,1,256,16]{2,3,1,0:T(8,128)} %param.10) | copy-start | bytes 393220
  320.7 27.7 %all-to-all-start = ((f32[32,256,16]{1,2,0:T(8,128)}), f32[32,256,16]{1,2,0:T(8,128)S(1)}, u32[]{:S(2)}, u32[]{:S(2)}) async-start(f32[32,256,16]{1,2,0:T(8,128)} %broadcast_in_dim.11), calls=%async_computation | async-start | bytes 1048576 | tf_op jit(solution)/shard_map/all_to_all | solution.py:25
  329.9 166.5 %all-gather.20.cloned.1.call-start = ((), (), s32[]{:S(2)}) async-start(), calls=%async_computation.6 | async-start | bytes 9437184 | tf_op jit(solution)/shard_map/all_gather | solution.py:40
  425.9 2.0 copy-start.2
  500.9 14.2 %copy-start.5 = (f32[4]{0:T(128)S(1)}, f32[4]{0:T(128)}, u32[]{:S(2)}) copy-start(f32[4]{0:T(128)} %param.11) | copy-start | bytes 52
  505.1 38.8 %all-to-all-start.1 = ((f32[2,256,32,16]{1,0,3,2:T(2,128)}), f32[2,256,32,16]{1,0,3,2:T(2,128)S(1)}, u32[]{:S(2)}, u32[]{:S(2)}) async-start(f32[2,256,32,16]{1,0,3,2:T(2,128)} %reshape.136), calls=%async_computation.1 | async-start | bytes 2097152 | tf_op jit(solution)/shard_map/all_to_all | solution.py:93
  517.2 27.6 %copy-start.1 = (f32[256,256]{1,0:T(8,128)S(1)}, f32[256,256]{1,0:T(8,128)}, u32[]{:S(2)}) copy-start(f32[256,256]{1,0:T(8,128)} %param.9) | copy-start | bytes 786436
  517.2 26.8 %copy-start.4 = (f32[8,256,16]{1,2,0:T(8,128)}, f32[8,256,16]{1,2,0:T(8,128)S(1)}, u32[]{:S(2)}) copy-start(f32[8,256,16]{1,2,0:T(8,128)S(1)} %fusion.4) | copy-start | bytes 393220
Sparse Core Ops, SparseCore 0:
  32.6 88.1 all-gather.11
  126.5 171.9 all-gather.13
  301.0 84.7 all-gather.17
  387.6 31.6 all-gather.15
  444.2 52.1 all-gather.19
